TPU v7x, 32 devices: a whole 2x2x4 slice. The times are simulated.
32 devices in a mesh: grp: 8 (over z, y), rep: 4 (over x, core).
Axes of the slice: x: 2, y: 2, z: 4, core: 2. Of those that a mesh axis runs over, the one named last changes fastest.
Arguments:
- queries: bfloat16 [16, 4, 32, 128], P('grp', 'rep'), may hold values from -3.2 to 3.2
- passages: bfloat16 [512, 4, 180, 128], P('grp', 'rep'), may hold values from -1.796875 to 1.796875
- lengths: int32 [512, 4], P('grp', 'rep'), may hold values from 16 to 180
- cand_ids: int32 [16, 4, 64], P('grp', 'rep'), may hold values from 0 to 511, as said below
- owner_map: int32 [4, 512], P('rep'), may hold values from 0 to 511, as said below
- teacher: float32 [16, 4, 64], P('grp', 'rep'), may hold values from -12 to 312
- weights: float32 [16, 4], P('grp', 'rep'), may hold values from 0.5 to 18
Outputs:
- loss: float32 [], replicated
- query_grad: float32 [16, 4, 32, 128], P('grp', 'rep')
- passage_grad: bfloat16 [512, 4, 180, 128], P('grp', 'rep')
Inputs may be any that keep to these rules, and one draw needn't show every extreme that they name: `cand_ids`: within each replica, the 128 candidates of the queries of one grp index have storage rows of which at most 32 (counted with repeats) lie in any one aligned block of 64 rows; in every draw, in each replica, one block receives exactly 32 from every grp index. `owner_map`: each row is a permutation of 0 to 511.
All inputs are finite; a program needn't handle non-finite values.
Results may differ from a plain program's by a relative error of at most 0.0055.
Values may be sent and summed in bfloat16 or wider, within the bound.
No kernel may reach another device: no remote copies, remote signals or barrier semaphores. Data moves between devices by JAX's collectives and lax.ppermute only.
A program may use at most 128 MiB of HBM per device.

v0:
```python
import jax
import jax.numpy as jnp
from jax import lax
from jax.sharding import PartitionSpec as P

temper = 0.05


def token_softmax(products, lengths_used):
    usable = (
        lax.broadcasted_iota(jnp.int32, products.shape, products.ndim - 1)
        < lengths_used[..., None, None]
    )
    scaled = jnp.where(usable, products / temper, -1e30)
    highest = jnp.max(scaled, axis=-1, keepdims=True)
    powers = jnp.where(usable, jnp.exp(scaled - highest), 0.0)
    summed = jnp.sum(powers, axis=-1, keepdims=True)
    matched = temper * (highest[..., 0] + jnp.log(summed[..., 0]))
    return (matched, powers / summed)


def on_device(queries, passages, lengths, cand_ids, owner_map, teacher, weights):
    groups = lax.axis_size("grp")
    replicas = lax.axis_size("rep")
    query_local = queries.shape[0]
    query_len = queries.shape[2]
    feature_dim = queries.shape[3]
    passage_local = passages.shape[0]
    token_len = passages.shape[2]
    candidates = cand_ids.shape[2]
    ref_count = query_local * candidates
    capacity = 2 * ref_count // groups
    slot_count = groups * capacity
    block_width = token_len * feature_dim
    query_width = query_len * feature_dim
    position_table = owner_map[0]
    wanted = cand_ids[:, 0, :].reshape(ref_count)
    table_index = jnp.arange(position_table.shape[0], dtype=jnp.int32)
    positions = jnp.sum(
        jnp.where(wanted[:, None] == table_index[None, :], position_table[None, :], 0), axis=1
    )
    owner_index = positions // passage_local
    local_row = positions % passage_local
    owner_hot = (owner_index[:, None] == jnp.arange(groups, dtype=jnp.int32)[None, :]).astype(
        jnp.int32
    )
    before = jnp.cumsum(owner_hot, axis=0) - owner_hot
    slot_rank = jnp.sum(before * owner_hot, axis=1)
    slot_index = owner_index * capacity + slot_rank
    request = jnp.full((slot_count,), -1, jnp.int32).at[slot_index].set(local_row)
    asked_rows = lax.all_to_all(
        request.reshape(groups, capacity), "grp", split_axis=0, concat_axis=0, tiled=True
    ).reshape(slot_count)
    present = asked_rows >= 0
    safe_rows = jnp.maximum(asked_rows, 0)
    slot_lengths = jnp.where(present, lengths[:, 0][safe_rows], 0)
    stored_index = jnp.arange(passage_local, dtype=jnp.int32)
    gather_hot = (asked_rows[None, :] == stored_index[:, None]).astype(jnp.bfloat16)
    pick_hot = (asked_rows[:, None] == stored_index[None, :]).astype(jnp.bfloat16)
    route_hot = (slot_index[:, None] == jnp.arange(slot_count, dtype=jnp.int32)[None, :]).astype(
        jnp.bfloat16
    )
    flat_passages = passages.reshape(passage_local, block_width)
    query_flat = queries[:, 0]
    query_weights = weights[:, 0]
    query_source = jnp.arange(ref_count, dtype=jnp.int32) // candidates
    blocks_flat = jnp.dot(pick_hot, flat_passages, preferred_element_type=jnp.float32).astype(
        jnp.bfloat16
    )
    ref_queries = query_flat[query_source].reshape(ref_count, query_width)
    slot_queries = jnp.einsum(
        "rs,rk->sk", route_hot, ref_queries, preferred_element_type=jnp.float32
    ).astype(jnp.bfloat16)
    got_queries = lax.all_to_all(
        slot_queries.reshape(groups, capacity, query_width),
        "grp",
        split_axis=0,
        concat_axis=0,
        tiled=True,
    )
    got_queries = got_queries.reshape(slot_count, query_len, feature_dim)
    blocks = blocks_flat.reshape(slot_count, token_len, feature_dim)
    products = jnp.einsum("sid,sjd->sij", got_queries, blocks, preferred_element_type=jnp.float32)
    matched, attention = token_softmax(products, jnp.maximum(slot_lengths, 1))
    slot_scores = jnp.sum(matched, axis=-1)
    back_scores = lax.all_to_all(
        slot_scores.reshape(groups, capacity), "grp", split_axis=0, concat_axis=0, tiled=True
    ).reshape(slot_count)
    student = back_scores[slot_index].reshape(query_local, candidates)
    log_student = jax.nn.log_softmax(student, axis=-1)
    log_teacher = jax.nn.log_softmax(teacher[:, 0], axis=-1)
    teacher_prob = jnp.exp(log_teacher)
    divergence = jnp.sum(teacher_prob * (log_teacher - log_student), axis=-1)
    totals = lax.psum((jnp.sum(query_weights * divergence), jnp.sum(query_weights)), ("grp", "rep"))
    loss_value = totals[0] / totals[1]
    scale_all = query_local * groups * replicas
    score_grad = (
        scale_all * query_weights[:, None] / totals[1] * (jnp.exp(log_student) - teacher_prob)
    )
    loss_value, score_grad = (loss_value, score_grad)
    slot_score_grad = (
        jnp.zeros((slot_count,), jnp.float32).at[slot_index].set(score_grad.reshape(ref_count))
    )
    arrived = lax.all_to_all(
        slot_score_grad.reshape(groups, capacity), "grp", split_axis=0, concat_axis=0, tiled=True
    ).reshape(slot_count)
    scaled_grad = (arrived[:, None, None] * attention).astype(jnp.bfloat16)
    pair_query = jnp.einsum(
        "sij,sjd->sid", scaled_grad, blocks, preferred_element_type=jnp.float32
    ).astype(jnp.bfloat16)
    returned_queries = lax.all_to_all(
        pair_query.reshape(groups, capacity, query_width),
        "grp",
        split_axis=0,
        concat_axis=0,
        tiled=True,
    )
    ordered = jnp.dot(
        route_hot,
        returned_queries.reshape(slot_count, query_width),
        preferred_element_type=jnp.float32,
    )
    query_grad = jnp.sum(ordered.reshape(query_local, candidates, query_len, feature_dim), axis=1)
    returned = jnp.einsum(
        "sij,sid->sjd", scaled_grad, got_queries, preferred_element_type=jnp.float32
    ).astype(jnp.bfloat16)
    returned = returned.reshape(slot_count, block_width)
    passage_sum = jnp.dot(gather_hot, returned, preferred_element_type=jnp.float32)
    passage_grad = passage_sum.astype(jnp.bfloat16).reshape(
        passage_local, 1, token_len, feature_dim
    )
    return (loss_value, query_grad[:, None], passage_grad)


def solution(mesh):
    return jax.shard_map(
        on_device,
        mesh=mesh,
        in_specs=(
            P("grp", "rep", None, None),
            P("grp", "rep", None, None),
            P("grp", "rep"),
            P("grp", "rep", None),
            P("rep", None),
            P("grp", "rep", None),
            P("grp", "rep"),
        ),
        out_specs=(P(), P("grp", "rep", None, None), P("grp", "rep", None, None)),
        check_vma=False,
    )
```

profile of v0, /device:TPU:0, one launch (start us, length us, event | category | flops | bytes accessed | tf_op | source)
XLA Modules:
  0.0 235.0 jit_solution(7812070350902260653)
XLA Ops:
  0.7 0.5 broadcast.316
  1.2 1.3 reduce.17
  2.6 0.9 select_reduce_fusion
  3.6 0.2 reduce_window_sum.11
  3.7 0.2 select_reduce_fusion.1
  3.9 1.0 scatter_custom_fusion
  4.9 0.7 all_to_all.24
  5.6 7.3 %all-to-all-start = ((s32[8,1,32]{2,1,0:T(1,128)}), s32[8,1,32]{2,1,0:T(1,128)S(1)}, u32[]{:S(2)}, u32[]{:S(2)}) async-start(s32[8,1,32]{2,1,0:T(1,128)} %all_to_all.24), calls=%async_computation | async-start | bytes 8192 | tf_op jit(solution)/shard_map/all_to_all | solution.py:51
  13.0 0.8 gather_fusion.1
  13.7 2.2 convolution_convert_fusion.3
  15.9 3.4 %all-to-all-done = s32[8,1,32]{2,1,0:T(1,128)S(1)} async-done(((s32[8,1,32]{2,1,0:T(1,128)}), s32[8,1,32]{2,1,0:T(1,128)S(1)}, u32[]{:S(2)}, u32[]{:S(2)}) %all-to-all-start) | async-done | bytes 1056 | tf_op jit(solution)/shard_map/all_to_all | solution.py:51
  19.3 4.4 %all-to-all-start.1 = ((bf16[8,32,4096]{2,1,0:T(8,128)(2,1)}), bf16[8,32,4096]{2,1,0:T(8,128)(2,1)}, u32[]{:S(2)}, u32[]{:S(2)}) async-start(bf16[8,32,4096]{2,1,0:T(8,128)(2,1)} %bitcast.9), calls=%async_computation.1 | async-start | bytes 4194304 | tf_op jit(solution)/shard_map/all_to_all | solution.py:74
  23.7 3.7 %copy.19 = bf16[64,1,180,128]{3,2,0,1:T(8,128)(2,1)S(1)} copy(bf16[64,1,180,128]{3,0,2,1:T(8,128)(2,1)} %param.9) | data formatting | bytes 5898240 | tf_op args[1]
  27.6 0.2 exponential_reduce_fusion.1
  27.8 0.7 maximum_reduce_fusion
  28.6 6.2 %convolution_convert_fusion = bf16[256,23040]{1,0:T(8,128)(2,1)} fusion(bf16[8,8,180,128]{3,2,1,0:T(8,128)(2,1)S(1)} %bitcast.67, s32[256]{0:T(256)S(1)} %reshape.239), kind=kOutput, calls=%fused_computation.5 | convolution fusion | flops 760889344 | bytes 14746624 | tf_op jit(solution)/shard_map/dot_general | solution.py:67
  34.8 16.2 %copy.20 = bf16[256,23040]{0,1:T(8,128)(2,1)} copy(bf16[256,23040]{1,0:T(8,128)(2,1)} %convolution_convert_fusion) | data formatting | bytes 23592960 | tf_op jit(solution)/shard_map/convert_element_type | solution.py:67
  51.0 16.5 %copy.21 = bf16[256,180,128]{2,1,0:T(8,128)(2,1)} copy(bf16[256,180,128]{0,2,1:T(8,128)(2,1)} %bitcast.66) | data formatting | bytes 23592960 | tf_op jit(solution)/shard_map/reshape | solution.py:82
  67.6 1.9 gather_fusion
  69.5 1.3 all-to-all-done.1
  70.8 2.1 copy.28
  72.9 15.2 %fusion = (f32[256,32]{1,0:T(8,128)S(1)}, f32[256,32,180]{2,1,0:T(8,128)}) fusion(s32[256]{0:T(256)S(1)} %fusion.13, bf16[256,32,128]{2,1,0:T(8,128)(2,1)S(1)} %bitcast.69, bf16[256,180,128]{2,1,0:T(8,128)(2,1)} %copy.21), kind=kOutput, calls=%fused_computation.12 | convolution fusion | flops 383377408 | bytes 19825664 | tf_op jit(solution)/shard_map/sid,sjd->sij/dot_general | solution.py:83
  88.1 6.4 %fusion.1 = f32[256,32]{1,0:T(8,128)S(1)} fusion(f32[256,32,180]{2,1,0:T(8,128)} %get-tuple-element.20, f32[256,32]{1,0:T(8,128)S(1)} %get-tuple-element.19, s32[256]{0:T(256)S(1)} %fusion.13), kind=kLoop, calls=%fused_computation.14 | loop fusion | flops 8839168 | bytes 5964800 | tf_op jit(solution)/shard_map/reduce_sum | solution.py:17
  94.7 0.7 all_to_all.27
  95.3 4.6 %all-to-all-start.2 = ((f32[8,1,32]{2,1,0:T(1,128)}), f32[8,1,32]{2,1,0:T(1,128)S(1)}, u32[]{:S(2)}, u32[]{:S(2)}) async-start(f32[8,1,32]{2,1,0:T(1,128)} %all_to_all.27), calls=%async_computation.2 | async-start | bytes 8192 | tf_op jit(solution)/shard_map/all_to_all | solution.py:86
  100.0 0.6 reduce_sum.97
  100.6 5.8 %all-to-all-done.2 = f32[8,1,32]{2,1,0:T(1,128)S(1)} async-done(((f32[8,1,32]{2,1,0:T(1,128)}), f32[8,1,32]{2,1,0:T(1,128)S(1)}, u32[]{:S(2)}, u32[]{:S(2)}) %all-to-all-start.2) | async-done | bytes 1056 | tf_op jit(solution)/shard_map/all_to_all | solution.py:86
  106.3 0.5 broadcast.318
  106.9 0.7 reduce.19
  107.6 1.3 gather_fusion.2
  109.1 0.2 exponential_reduce_fusion
  109.3 0.2 multiply_reduce_fusion.1
  109.5 0.6 fusion.16
  110.1 38.7 %all-reduce = (f32[]{:T(128)}, f32[]{:T(128)}) all-reduce(f32[]{:T(128)} %fusion.16, f32[]{:T(128)} %reduce_sum.97), channel_id=1, replica_groups=mesh['grp'=8,'rep'=4] {'grp','rep'}, use_global_device_ids=true, to_apply=%region_11.13 | all-reduce | flops 2 | bytes 16 | tf_op jit(solution)/shard_map/psum | solution.py:94
  148.8 0.7 divide_bitcast_fusion
  149.6 1.0 scatter_custom_fusion.1
  150.7 11.1 %all_to_all.37 = f32[8,1,32]{2,1,0:T(1,128)S(1)} all-to-all(f32[8,1,32]{2,1,0:T(1,128)S(1)} %all_to_all.29), channel_id=1, replica_groups=mesh['grp'=8,'rep'=4] {'grp'}, dimensions={0} | all-to-all | bytes 2048 | tf_op jit(solution)/shard_map/all_to_all | solution.py:104
  161.8 0.7 reduce.20
  162.5 10.3 %convolution_convert_fusion.4 = bf16[256,32,128]{2,1,0:T(8,128)(2,1)} fusion(bf16[256,180,128]{2,1,0:T(8,128)(2,1)} %copy.21, f32[256,32,180]{2,1,0:T(8,128)} %get-tuple-element.20, f32[256,32]{1,0:T(8,128)S(1)} %fusion.1, f32[256]{0:T(256)S(1)} %mul.78, f32[256,32]{1,0:T(8,128)S(1)} %get-tuple-element.19, s32[256]{0:T(256)S(1)} %fusion.13), kind=kOutput, calls=%fused_computation.17 | convolution fusion | flops 390332416 | bytes 19859456 | tf_op jit(solution)/shard_map/sij,sjd->sid/dot_general | solution.py:108
  172.8 4.2 %reshape.248 = bf16[8,32,4096]{2,1,0:T(8,128)(2,1)} reshape(bf16[256,32,128]{2,1,0:T(8,128)(2,1)} %convolution_convert_fusion.4) | data formatting | bytes 4194304 | tf_op jit(solution)/shard_map/reshape | solution.py:112
  177.0 4.4 %all-to-all-start.4 = ((bf16[8,32,4096]{2,1,0:T(8,128)(2,1)}), bf16[8,32,4096]{2,1,0:T(8,128)(2,1)}, u32[]{:S(2)}, u32[]{:S(2)}) async-start(bf16[8,32,4096]{2,1,0:T(8,128)(2,1)} %reshape.248), calls=%async_computation.4 | async-start | bytes 4194304 | tf_op jit(solution)/shard_map/all_to_all | solution.py:111
  182.9 14.7 %convolution_convert_fusion.2 = bf16[256,180,128]{2,1,0:T(8,128)(2,1)} fusion(bf16[256,32,128]{2,1,0:T(8,128)(2,1)S(1)} %bitcast.70, f32[256,32,180]{2,1,0:T(8,128)} %get-tuple-element.20, f32[256,32]{1,0:T(8,128)S(1)} %fusion.1, f32[256]{0:T(256)S(1)} %mul.78, f32[256,32]{1,0:T(8,128)S(1)} %get-tuple-element.19, s32[256]{0:T(256)S(1)} %fusion.13), kind=kOutput, calls=%fused_computation.11 | convolution fusion | flops 395182080 | bytes 19859456 | tf_op jit(solution)/shard_map/sij,sid->sjd/dot_general | solution.py:124
  197.6 16.4 %copy.24 = bf16[256,180,128]{0,2,1:T(8,128)(2,1)} copy(bf16[256,180,128]{2,1,0:T(8,128)(2,1)} %convolution_convert_fusion.2) | data formatting | bytes 23592960 | tf_op jit(solution)/shard_map/convert_element_type | solution.py:126
  214.0 8.0 %convolution_convert_fusion.1 = bf16[64,23040]{1,0:T(8,128)(2,1)S(1)} fusion(bf16[256,23040]{0,1:T(8,128)(2,1)} %bitcast.65, s32[256]{0:T(256)S(1)} %reshape.239), kind=kOutput, calls=%fused_computation.6 | convolution fusion | flops 756465664 | bytes 14746624 | tf_op jit(solution)/shard_map/dot_general | solution.py:128
  222.0 2.9 %reshape.251 = bf16[64,1,180,128]{3,2,0,1:T(8,128)(2,1)} reshape(bf16[64,23040]{1,0:T(8,128)(2,1)S(1)} %convolution_convert_fusion.1) | data formatting | bytes 5898240 | tf_op jit(solution)/shard_map/reshape | solution.py:129
  224.9 4.2 %copy.25 = bf16[64,1,180,128]{3,0,2,1:T(8,128)(2,1)} copy(bf16[64,1,180,128]{3,2,0,1:T(8,128)(2,1)} %reshape.251) | data formatting | bytes 5898240
  229.2 3.3 %copy.23 = bf16[256,4096]{0,1:T(8,128)(2,1)S(1)} copy(bf16[256,4096]{1,0:T(8,128)(2,1)} %bitcast.15) | data formatting | bytes 4194304 | tf_op jit(solution)/shard_map/reshape | solution.py:120
  232.4 1.4 convolution_reduce_fusion
  (37 shorter events, 1.5 us)
Async XLA Ops:
  0.6 12.3 %copy-start = (bf16[2,1,32,128]{3,2,1,0:T(8,128)(2,1)S(1)}, bf16[2,1,32,128]{3,2,1,0:T(8,128)(2,1)}, u32[]{:S(2)}) copy-start(bf16[2,1,32,128]{3,2,1,0:T(8,128)(2,1)} %param.8) | copy-start | bytes 49156
  0.6 26.8 %copy-start.3 = (f32[2,1,64]{2,1,0:T(1,128)S(1)}, f32[2,1,64]{2,1,0:T(1,128)}, u32[]{:S(2)}) copy-start(f32[2,1,64]{2,1,0:T(1,128)} %param.13) | copy-start | bytes 1540
  5.6 13.7 %all-to-all-start = ((s32[8,1,32]{2,1,0:T(1,128)}), s32[8,1,32]{2,1,0:T(1,128)S(1)}, u32[]{:S(2)}, u32[]{:S(2)}) async-start(s32[8,1,32]{2,1,0:T(1,128)} %all_to_all.24), calls=%async_computation | async-start | bytes 8192 | tf_op jit(solution)/shard_map/all_to_all | solution.py:51
  19.3 51.5 %all-to-all-start.1 = ((bf16[8,32,4096]{2,1,0:T(8,128)(2,1)}), bf16[8,32,4096]{2,1,0:T(8,128)(2,1)}, u32[]{:S(2)}, u32[]{:S(2)}) async-start(bf16[8,32,4096]{2,1,0:T(8,128)(2,1)} %bitcast.9), calls=%async_computation.1 | async-start | bytes 4194304 | tf_op jit(solution)/shard_map/all_to_all | solution.py:74
  51.0 16.5 %copy-start.2 = (s32[64,1]{0,1:T(1,128)S(1)}, s32[64,1]{0,1:T(1,128)}, u32[]{:S(2)}) copy-start(s32[64,1]{0,1:T(1,128)} %param.10) | copy-start | bytes 772
  88.1 11.9 %copy-start.4 = (f32[2,1]{0,1:T(1,128)S(1)}, f32[2,1]{0,1:T(1,128)}, u32[]{:S(2)}) copy-start(f32[2,1]{0,1:T(1,128)} %param.14) | copy-start | bytes 28
  95.3 11.0 %all-to-all-start.2 = ((f32[8,1,32]{2,1,0:T(1,128)}), f32[8,1,32]{2,1,0:T(1,128)S(1)}, u32[]{:S(2)}, u32[]{:S(2)}) async-start(f32[8,1,32]{2,1,0:T(1,128)} %all_to_all.27), calls=%async_computation.2 | async-start | bytes 8192 | tf_op jit(solution)/shard_map/all_to_all | solution.py:86
  177.0 52.1 %all-to-all-start.4 = ((bf16[8,32,4096]{2,1,0:T(8,128)(2,1)}), bf16[8,32,4096]{2,1,0:T(8,128)(2,1)}, u32[]{:S(2)}, u32[]{:S(2)}) async-start(bf16[8,32,4096]{2,1,0:T(8,128)(2,1)} %reshape.248), calls=%async_computation.4 | async-start | bytes 4194304 | tf_op jit(solution)/shard_map/all_to_all | solution.py:111
  214.0 19.8 %copy-start.1 = (bf16[2,1,32,128]{3,2,1,0:T(8,128)(2,1)S(1)}, bf16[2,1,32,128]{3,2,1,0:T(8,128)(2,1)}, u32[]{:S(2)}) copy-start(bf16[2,1,32,128]{3,2,1,0:T(8,128)(2,1)} %param.8) | copy-start | bytes 49156
where the time goes:
time: 237 us; the launch traced here: 235 us
  local copies, waits for them, and re-layouts  78.6 us (33%)
  matrix products  58 us (24%)
  blocking collectives  49.8 us (21%)
  starting transfers between devices  20.6 us (9%)
  other arithmetic  14 us (6%)
  waiting for transfers between devices  10.6 us (4%)
  between operations  3.39 us (1%)
    psum x1, blocking collectives, on_device(): lax.psum((jnp.sum(query_weights * divergence), jnp.sum(query_weights)), (...  38.7 us
    reshape x1, local copies, waits for them, and re-layouts, on_device(): blocks = blocks_flat.reshape(slot_count, token_len, feature_dim)  16.5 us
    convert_element_type x1, local copies, waits for them, and re-layouts, on_device(): returned = jnp.einsum('sij,sid->sjd', scaled_grad, got_queries, preferred...  16.4 us
    convert_element_type x1, local copies, waits for them, and re-layouts, on_device(): jnp.dot(pick_hot, flat_passages, preferred_element_type=jnp.float32)  16.2 us
    dot_general x1, matrix products, on_device(): jnp.einsum('sid,sjd->sij', got_queries, blocks, preferred_element_type=jn...  15.2 us
    dot_general x1, matrix products, on_device(): jnp.einsum('sij,sid->sjd', scaled_grad, got_queries, preferred_element_ty...  14.7 us
    all_to_all x1, blocking collectives, on_device(): lax.all_to_all(slot_score_grad.reshape(groups, capacity), 'grp', split_ax...  11.1 us
    unnamed x14, local copies, waits for them, and re-layouts  10.6 us
  transfers between devices with their start and end apart: 4, of which 3 were waited for; matrix products, arithmetic and copies ran while one was open for 41% of the time, Pallas kernels for 0%

commit v1 on v0

v1 whole, which is shorter than its diff:
```python
import functools
import math

import jax
import jax.numpy as jnp
from jax import lax
from jax.experimental import pallas as pl
from jax.experimental.pallas import tpu as pltpu
from jax.sharding import PartitionSpec as P

TEMPER = 0.05
LOG2E = math.log2(math.e)
MASKED = -1e30
KINDS = 8
UNROLL = 4
HIGHEST = lax.Precision.HIGHEST
VMEM = pltpu.VMEM
SMEM = pltpu.SMEM


def round_up(value, multiple):
    return -(-value // multiple) * multiple


def iota(shape, dim):
    return lax.broadcasted_iota(jnp.int32, shape, dim)


def three_parts(values):
    first = values.astype(jnp.bfloat16).astype(jnp.float32)
    rest = values - first
    second = rest.astype(jnp.bfloat16).astype(jnp.float32)
    third = (rest - second).astype(jnp.bfloat16).astype(jnp.float32)
    return first, second, third


def pack_kernel(passage_local, queries, cand_ids, owner_map, teacher, weights, out, aux):
    groups = out.shape[0]
    tokens = queries.shape[0]
    query_local, _, candidates = cand_ids.shape
    entries = owner_map.shape[1]
    table = owner_map[...].astype(jnp.float32)
    owner = jnp.floor((table + 0.5) * (1.0 / passage_local))
    local = table - owner * passage_local
    which = iota((8, entries), 0)
    tables = jnp.where(which == 0, owner, jnp.where(which == 1, local, 0.0)).astype(jnp.bfloat16)
    aux[...] = jnp.zeros_like(aux)
    for q in range(query_local):
        hot = (iota((entries, candidates), 0) == cand_ids[q]).astype(jnp.bfloat16)
        found = jnp.dot(tables, hot, preferred_element_type=jnp.float32)
        scores = teacher[q]
        shifted = scores - jnp.max(scores, axis=1, keepdims=True)
        log_teacher = shifted - jnp.log(jnp.sum(jnp.exp(shifted), axis=1, keepdims=True))
        weight = jnp.broadcast_to(weights[:, q : q + 1], (1, candidates))
        rows = (found[0:1], found[1:2], *three_parts(log_teacher), *three_parts(weight))
        for kind, row in enumerate(rows):
            at = kind * query_local + q
            aux[at : at + 1, 0:candidates] = row
    packed = aux[...].astype(jnp.bfloat16)
    for g in range(groups):
        out[g, 0:tokens, :] = queries[...]
        out[g, tokens:, :] = packed


def owned_rows(arrived, tokens, query_local, candidates, g, q, me):
    at = tokens + q
    owner = arrived[g, at : at + 1, 0:candidates].astype(jnp.float32)
    at = tokens + query_local + q
    local = arrived[g, at : at + 1, 0:candidates].astype(jnp.float32)
    return jnp.where(owner == me.astype(jnp.float32), local, -1.0).astype(jnp.int32)


def score_kernel(
    dims,
    count_axis,
    arrived,
    passages,
    lengths,
    weight_sums,
    scores_out,
    powers,
    inverse,
    block_row,
    block_tile,
    block_count,
    turned,
    matched,
    flags,
    flags_scalar,
    copy_done,
):
    tokens, query_local, candidates, per_tile = dims
    groups = arrived.shape[0]
    passage_count, padded, feature = passages.shape
    tiles = turned.shape[0]
    me = lax.axis_index(count_axis)
    groups_per_tile = per_tile // query_local

    column = iota(flags.shape, 1)
    passage_index = iota((passage_count, candidates), 0)
    marks = jnp.zeros(flags.shape, jnp.int32)
    for tile in range(tiles):
        hit = jnp.zeros((passage_count, candidates), jnp.int32)
        for g in range(tile * groups_per_tile, (tile + 1) * groups_per_tile):
            for q in range(query_local):
                mine = owned_rows(arrived, tokens, query_local, candidates, g, q, me)
                hit = jnp.where(passage_index == mine, 1, hit)
        any_hit = jnp.max(hit, axis=1, keepdims=True)
        marks = jnp.where(column == tile, any_hit, marks)
    flags[...] = marks
    to_scalar = pltpu.make_async_copy(flags, flags_scalar, copy_done)
    to_scalar.start()

    for tile in range(tiles):
        parts = [
            arrived[g, 0:tokens, :]
            for g in range(tile * groups_per_tile, (tile + 1) * groups_per_tile)
        ]
        block = jnp.concatenate(parts, axis=0).astype(jnp.float32)
        turned[tile] = block.T.astype(jnp.bfloat16)
    matched[...] = jnp.zeros_like(matched)
    inverse[...] = jnp.zeros_like(inverse)
    to_scalar.wait()

    def list_passage(p, count):
        for tile in range(tiles):
            block_row[0, count] = p
            block_tile[0, count] = tile
            count = count + flags_scalar[p, tile]
        return count

    count = lax.fori_loop(0, passage_count, list_passage, jnp.int32(0))
    for extra in range(UNROLL):
        block_row[0, count + extra] = passage_count
        block_tile[0, count + extra] = 0
    steps = (count + UNROLL - 1) // UNROLL
    block_count[0, 0] = steps

    token_index = iota((padded, feature), 0)
    factor = LOG2E / TEMPER

    def step(s, carry):
        for u in range(UNROLL):
            b = s * UNROLL + u
            slot = block_row[0, b]
            tile = block_tile[0, b]
            p = jnp.minimum(slot, passage_count - 1)
            products = jnp.dot(passages[p], turned[tile], preferred_element_type=jnp.float32)
            products = jnp.where(token_index < lengths[0, p], products, MASKED)
            highest = jnp.max(products, axis=0, keepdims=True)
            raised = jnp.exp2((products - highest) * factor)
            summed = jnp.sum(raised, axis=0, keepdims=True)
            powers[b] = raised.astype(jnp.bfloat16)
            matched[tile, pl.ds(slot, 1), :] = highest + TEMPER * jnp.log(summed)
            inverse[tile, pl.ds(slot, 1), :] = 1.0 / summed
        return carry

    lax.fori_loop(0, steps, step, 0)

    lanes = matched.shape[2]
    query_len = lanes // per_tile
    member = iota((lanes, 128), 0) // query_len == iota((lanes, 128), 1)
    member = member.astype(jnp.float32)
    for tile in range(tiles):
        sums = jnp.dot(
            matched[tile, 0:passage_count, :],
            member,
            precision=HIGHEST,
            preferred_element_type=jnp.float32,
        )
        for inner in range(per_tile):
            g = tile * groups_per_tile + inner // query_local
            q = inner % query_local
            mine = owned_rows(arrived, tokens, query_local, candidates, g, q, me)
            column = sums[:, inner : inner + 1]
            picked = jnp.where(passage_index == mine, column, 0.0)
            row = jnp.sum(picked, axis=0, keepdims=True)
            at = tile * per_tile + inner
            scores_out[0, at : at + 1, :] = row
    queries_all = tiles * per_tile
    total = jnp.sum(weight_sums[...], axis=1, keepdims=True)
    scores_out[0, queries_all:, :] = jnp.broadcast_to(
        total, (scores_out.shape[1] - queries_all, candidates)
    )
    for g in range(1, groups):
        scores_out[g] = scores_out[0]


def query_kernel(
    dims,
    count_axis,
    arrived,
    scores,
    passages,
    inverse,
    powers,
    block_row,
    block_tile,
    block_count,
    grads_out,
    scaled,
    loss_parts,
    multiplier,
    sums,
):
    tokens, query_local, candidates, per_tile, query_total = dims
    groups = arrived.shape[0]
    passage_count, padded, feature = passages.shape
    tiles, _, lanes = inverse.shape
    groups_per_tile = per_tile // query_local
    queries_all = tiles * per_tile
    query_len = lanes // per_tile
    me = lax.axis_index(count_axis)

    got = scores[0]
    for g in range(1, groups):
        got = got + scores[g]
    student = got[0:queries_all]
    weight_sum = got[queries_all : queries_all + 1, 0:1]

    def gather_parts(kind):
        rows = []
        for g in range(groups):
            parts = []
            for part in range(3):
                at = tokens + (kind + part) * query_local
                block = arrived[g, at : at + query_local, 0:candidates]
                parts.append(block.astype(jnp.float32))
            rows.append((parts[0] + parts[1]) + parts[2])
        return jnp.concatenate(rows, axis=0)

    log_teacher = gather_parts(2)
    weight = gather_parts(5)
    shifted = student - jnp.max(student, axis=1, keepdims=True)
    log_student = shifted - jnp.log(jnp.sum(jnp.exp(shifted), axis=1, keepdims=True))
    teacher_prob = jnp.exp(log_teacher)
    spread = jnp.sum(weight * teacher_prob * (log_teacher - log_student), axis=1, keepdims=True)
    numerator = jnp.sum(spread, axis=0, keepdims=True)
    half = iota(loss_parts.shape, 0)
    loss_parts[...] = jnp.where(half == 0, numerator, weight_sum)
    grad = (query_total * weight / weight_sum) * (jnp.exp(log_student) - teacher_prob)

    passage_index = iota((passage_count, candidates), 0)
    lane_query = iota((passage_count, lanes), 1) // query_len
    multiplier[...] = jnp.zeros_like(multiplier)
    for tile in range(tiles):
        spread_out = jnp.zeros((passage_count, lanes), jnp.float32)
        for inner in range(per_tile):
            g = tile * groups_per_tile + inner // query_local
            q = inner % query_local
            mine = owned_rows(arrived, tokens, query_local, candidates, g, q, me)
            at = tile * per_tile + inner
            picked = jnp.where(passage_index == mine, grad[at : at + 1], 0.0)
            column = jnp.sum(picked, axis=1, keepdims=True)
            spread_out = jnp.where(lane_query == inner, column, spread_out)
        multiplier[tile, 0:passage_count, :] = spread_out * inverse[tile, 0:passage_count, :]

    sums[...] = jnp.zeros_like(sums)

    def step(s, carry):
        for u in range(UNROLL):
            b = s * UNROLL + u
            slot = block_row[0, b]
            tile = block_tile[0, b]
            p = jnp.minimum(slot, passage_count - 1)
            part = powers[b].astype(jnp.float32) * multiplier[tile, pl.ds(slot, 1), :]
            part = part.astype(jnp.bfloat16)
            scaled[b] = part
            sums[tile] += lax.dot_general(
                passages[p], part, (((0,), (0,)), ((), ())), preferred_element_type=jnp.float32
            )
        return carry

    lax.fori_loop(0, block_count[0, 0], step, 0)
    for tile in range(tiles):
        turned = sums[tile].T.astype(jnp.bfloat16)
        for inner in range(groups_per_tile):
            g = tile * groups_per_tile + inner
            grads_out[g] = turned[inner * tokens : (inner + 1) * tokens]


def passage_kernel(
    dims, arrived, scaled, block_row, block_tile, block_count, out, sums, queries_all
):
    tokens, per_tile_groups = dims
    passage_count, token_len, _ = out.shape
    tiles = queries_all.shape[0]
    for tile in range(tiles):
        for inner in range(per_tile_groups):
            g = tile * per_tile_groups + inner
            queries_all[tile, inner * tokens : (inner + 1) * tokens, :] = arrived[g, 0:tokens, :]

    def clear(p, carry):
        sums[p] = jnp.zeros(sums.shape[1:], jnp.float32)
        return carry

    lax.fori_loop(0, passage_count, clear, 0)

    def step(s, carry):
        for u in range(UNROLL):
            b = s * UNROLL + u
            slot = block_row[0, b]
            sums[slot] += jnp.dot(
                scaled[b], queries_all[block_tile[0, b]], preferred_element_type=jnp.float32
            )
        return carry

    lax.fori_loop(0, block_count[0, 0], step, 0)

    def finish(p, carry):
        out[p] = sums[p, 0:token_len, :].astype(out.dtype)
        return carry

    lax.fori_loop(0, passage_count, finish, 0)


def vmem(count):
    return [pl.BlockSpec(memory_space=VMEM)] * count


def smem(count):
    return [pl.BlockSpec(memory_space=SMEM)] * count


def on_device(queries, passages, lengths, cand_ids, owner_map, teacher, weights):
    groups = lax.axis_size("grp")
    replicas = lax.axis_size("rep")
    query_local, _, query_len, feature = queries.shape
    passage_local, _, token_len, _ = passages.shape
    candidates = cand_ids.shape[2]
    tokens = query_local * query_len
    lanes = 128
    per_tile = lanes // query_len
    tiles = groups * tokens // lanes
    padded = round_up(token_len, 16)
    ref_count = query_local * candidates
    capacity = groups * (2 * ref_count // groups)
    blocks = min(passage_local * tiles, capacity) + UNROLL
    aux_rows = round_up(KINDS * query_local, 16)
    slots = round_up(passage_local + 1, 8)
    score_rows = round_up(groups * query_local + 1, 8)
    params = pltpu.CompilerParams
    shape = jax.ShapeDtypeStruct

    weight_row = weights.T
    share = pl.pallas_call(
        functools.partial(pack_kernel, passage_local),
        out_shape=shape((groups, tokens + aux_rows, feature), jnp.bfloat16),
        in_specs=vmem(5),
        out_specs=pl.BlockSpec(memory_space=VMEM),
        scratch_shapes=[VMEM((aux_rows, feature), jnp.float32)],
        name="pack",
    )(queries.reshape(tokens, feature), cand_ids, owner_map, teacher, weight_row)
    arrived = lax.all_to_all(share, "grp", split_axis=0, concat_axis=0, tiled=True)

    weight_sums = weight_row
    hop = 1
    while hop < replicas:
        ring = [(r, r ^ hop) for r in range(replicas)]
        weight_sums = weight_sums + lax.ppermute(weight_sums, "rep", ring)
        hop *= 2

    rows = jnp.pad(passages[:, 0], ((0, 0), (0, padded - token_len), (0, 0)))

    dims = (tokens, query_local, candidates, per_tile)
    scores, powers, inverse, block_row, block_tile, block_count = pl.pallas_call(
        functools.partial(score_kernel, dims, "grp"),
        out_shape=(
            shape((groups, score_rows, candidates), jnp.float32),
            shape((blocks, padded, lanes), jnp.bfloat16),
            shape((tiles, slots, lanes), jnp.float32),
            shape((1, blocks), jnp.int32),
            shape((1, blocks), jnp.int32),
            shape((1, 1), jnp.int32),
        ),
        in_specs=vmem(2) + smem(1) + vmem(1),
        out_specs=tuple(vmem(3) + smem(3)),
        scratch_shapes=[
            VMEM((tiles, feature, lanes), jnp.bfloat16),
            VMEM((tiles, slots, lanes), jnp.float32),
            VMEM((passage_local, 128), jnp.int32),
            SMEM((passage_local, 128), jnp.int32),
            pltpu.SemaphoreType.DMA,
        ],
        name="score",
    )(arrived, rows, lengths.T, weight_sums)
    all_scores = lax.all_to_all(scores, "grp", split_axis=0, concat_axis=0, tiled=True)

    query_total = query_local * groups * replicas
    grads, scaled, loss_parts = pl.pallas_call(
        functools.partial(query_kernel, dims + (query_total,), "grp"),
        out_shape=(
            shape((groups, tokens, feature), jnp.bfloat16),
            shape((blocks, padded, lanes), jnp.bfloat16),
            shape((8, 128), jnp.float32),
        ),
        in_specs=vmem(5) + smem(3),
        out_specs=tuple(vmem(3)),
        scratch_shapes=[
            VMEM((tiles, slots, lanes), jnp.float32),
            VMEM((tiles, feature, lanes), jnp.float32),
        ],
        input_output_aliases={4: 1},
        name="query_grad",
    )(arrived, all_scores, rows, inverse, powers, block_row, block_tile, block_count)
    returned = lax.all_to_all(grads, "grp", split_axis=0, concat_axis=0, tiled=True)

    passage_grad = pl.pallas_call(
        functools.partial(passage_kernel, (tokens, per_tile // query_local)),
        out_shape=shape((passage_local, token_len, feature), jnp.bfloat16),
        in_specs=vmem(2) + smem(3),
        out_specs=pl.BlockSpec(memory_space=VMEM),
        scratch_shapes=[
            VMEM((passage_local + 1, padded, feature), jnp.float32),
            VMEM((tiles, lanes, feature), jnp.bfloat16),
        ],
        name="passage_grad",
    )(arrived, scaled, block_row, block_tile, block_count)

    numerator = loss_parts[0:1, 0:1]
    weight_sum = loss_parts[1, 0]
    hop = 1
    while hop < replicas:
        ring = [(r, r ^ hop) for r in range(replicas)]
        numerator = numerator + lax.ppermute(numerator, "rep", ring)
        hop *= 2
    loss = numerator[0, 0] / weight_sum
    query_grad = jnp.sum(returned.astype(jnp.float32), axis=0)
    query_grad = query_grad.reshape(query_local, 1, query_len, feature)
    return (loss, query_grad, passage_grad[:, None])


def solution(mesh):
    return jax.shard_map(
        on_device,
        mesh=mesh,
        in_specs=(
            P("grp", "rep", None, None),
            P("grp", "rep", None, None),
            P("grp", "rep"),
            P("grp", "rep", None),
            P("rep", None),
            P("grp", "rep", None),
            P("grp", "rep"),
        ),
        out_specs=(P(), P("grp", "rep", None, None), P("grp", "rep", None, None)),
        check_vma=False,
    )
```

time: 237 us -> 110 us (0.46)
  local copies, waits for them, and re-layouts: 78.6 us -> 14.3 us
  matrix products: 58 us -> 0 us
  Pallas kernels: 0 us -> 49.3 us
  blocking collectives: 49.8 us -> 15.6 us
  other arithmetic: 14 us -> 1.91 us
  waiting for transfers between devices: 10.6 us -> 2.45 us
    dot_general x7 -> x0, matrix products: 58 us -> none  [the longest x1 15.2 us: on_device(): jnp.einsum('sid,sjd->sij', got_queries, blocks, preferred_element_type=jn...]
    pallas_call x0 -> x4, Pallas kernels: none -> 49.3 us  [the longest x1 18.4 us: on_device(): pl.pallas_call(functools.partial(query_kernel, dims + (query_total,), 'gr...]
    psum x1 -> x0, blocking collectives: 38.7 us -> none  [on_device(): lax.psum((jnp.sum(query_weights * divergence), jnp.sum(query_weights)), (...]
    convert_element_type x2 -> x0, local copies, waits for them, and re-layouts: 32.7 us -> none  [the longest x1 16.4 us: on_device(): returned = jnp.einsum('sij,sid->sjd', scaled_grad, got_queries, preferred...]
    reshape x8 -> x0, local copies, waits for them, and re-layouts: 27.2 us -> none  [the longest x1 16.5 us: on_device(): blocks = blocks_flat.reshape(slot_count, token_len, feature_dim)]
    all_to_all x4 -> x2, waiting for transfers between devices: 10.6 us -> 0.01 us  [the longest x1 0.01 us: on_device(): lax.all_to_all(share, 'grp', split_axis=0, concat_axis=0, tiled=True)]
    reduce_sum x9 -> x1, other arithmetic: 9.35 us -> 0.64 us  [on_device(): query_grad = jnp.sum(returned.astype(jnp.float32), axis=0)]
    ppermute x0 -> x4, starting transfers between devices: none -> 7.65 us  [the longest x2 6.09 us: on_device(): numerator = numerator + lax.ppermute(numerator, 'rep', ring)]
  transfers between devices with their start and end apart: 4 -> 6, of which waited for: 3 -> 2; matrix products, arithmetic and copies ran while one was open for 41% -> 11% of each run, Pallas kernels for 0% -> 12%
where the time goes in v1:
time: 110 us; the launch traced here: 109 us
  Pallas kernels  49.3 us (45%)
  starting transfers between devices  21.4 us (19%)
  blocking collectives  15.6 us (14%)
  local copies, waits for them, and re-layouts  14.3 us (13%)
  between operations  4.4 us (4%)
  waiting for transfers between devices  2.45 us (2%)
  other arithmetic  1.91 us (2%)
    pallas_call x1, Pallas kernels, on_device(): pl.pallas_call(functools.partial(query_kernel, dims + (query_total,), 'gr...  18.4 us
    pallas_call x1, Pallas kernels, on_device(): pl.pallas_call(functools.partial(score_kernel, dims, 'grp'), out_shape=(s...  16.2 us
    all_to_all x1, blocking collectives, on_device(): lax.all_to_all(scores, 'grp', split_axis=0, concat_axis=0, tiled=True)  15.6 us
    pallas_call x1, Pallas kernels, on_device(): pl.pallas_call(functools.partial(passage_kernel, (tokens, per_tile // que...  13.1 us
    unnamed x8, local copies, waits for them, and re-layouts  10.4 us
    all_to_all x1, starting transfers between devices, on_device(): lax.all_to_all(share, 'grp', split_axis=0, concat_axis=0, tiled=True)  7.31 us
    all_to_all x1, starting transfers between devices, on_device(): lax.all_to_all(grads, 'grp', split_axis=0, concat_axis=0, tiled=True)  6.42 us
    ppermute x2, starting transfers between devices, on_device(): numerator = numerator + lax.ppermute(numerator, 'rep', ring)  6.09 us
  transfers between devices with their start and end apart: 6, of which 2 were waited for; matrix products, arithmetic and copies ran while one was open for 11% of the time, Pallas kernels for 12%

profile of v1, /device:TPU:0, one launch (start us, length us, event | category | flops | bytes accessed | tf_op | source)
XLA Modules:
  0.0 109.4 jit_solution(10231171086037722752)
XLA Ops:
  0.6 1.6 %pack.1 = bf16[8,80,128]{2,1,0:T(8,128)(2,1)} custom-call(bf16[64,128]{1,0:T(8,128)(2,1)} %bitcast.13, s32[2,1,64]{2,1,0:T(1,128)} %cand_ids.1, s32[1,512]{1,0:T(1,128)} %owner_map.1, f32[2,1,64]{2,1,0:T(1,128)} %teacher.1, f32[1,2]{1,0:T(1,128)} %bitcast.14), custom_call_target="tpu_custom_call" | custom-call | tf_op jit(solution)/shard_map/pack/pallas_call | solution.py:346
  2.2 7.3 %all-to-all-start = ((bf16[8,80,128]{2,1,0:T(8,128)(2,1)}), bf16[8,80,128]{2,1,0:T(8,128)(2,1)S(1)}, u32[]{:S(2)}, u32[]{:S(2)}) async-start(bf16[8,80,128]{2,1,0:T(8,128)(2,1)} %pack.1), calls=%async_computation | async-start | bytes 327680 | tf_op jit(solution)/shard_map/all_to_all | solution.py:354
  9.5 0.0 collective-permute-start
  9.6 3.7 %copy.14 = bf16[64,1,180,128]{3,2,0,1:T(8,128)(2,1)S(1)} copy(bf16[64,1,180,128]{3,0,2,1:T(8,128)(2,1)} %param.8) | data formatting | bytes 5898240 | tf_op args[1]
  13.3 0.0 copy-start.1
  13.3 2.1 %pad.4.passages = bf16[64,192,128]{2,1,0:T(8,128)(2,1)} pad(bf16[64,180,128]{2,1,0:T(8,128)(2,1)S(1)} %bitcast.11, bf16[]{:T(256)} %constant.1.clone.1), padding=0_0x0_12x0_0 | pad | bytes 6094850 | tf_op jit(solution)/shard_map/jit(_pad)/pad | solution.py:363
  15.4 0.0 collective-permute-done
  15.4 0.0 copy-done.1
  15.4 1.6 %collective-permute-start.1 = (f32[1,2]{1,0:T(1,128)S(1)}, f32[1,2]{1,0:T(1,128)S(1)}, u32[]{:S(2)}, u32[]{:S(2)}) collective-permute-start(f32[1,2]{1,0:T(1,128)S(1)} %bitcast_add_fusion), channel_id=1, source_target_pairs={{0,2},{1,3},{2,0},{3,1},{4,6},{5,7},{6,4},{7,5},{8,10},{9,11},{10,... | collective-permute-start | bytes 32 | tf_op jit(solution)/shard_map/ppermute | solution.py:360
  17.0 2.1 %collective-permute-done.1 = f32[1,2]{1,0:T(1,128)S(1)} collective-permute-done((f32[1,2]{1,0:T(1,128)S(1)}, f32[1,2]{1,0:T(1,128)S(1)}, u32[]{:S(2)}, u32[]{:S(2)}) %collective-permute-start.1) | collective-permute-done | bytes 40 | tf_op jit(solution)/shard_map/ppermute | solution.py:360
  19.1 0.5 add.15.weight_sums
  19.6 0.0 all-to-all-done.arrived
  19.6 0.0 copy-start
  19.6 0.7 copy-done
  20.3 16.2 %score.1 = (f32[8,24,64]{2,1,0:T(8,128)}, bf16[260,192,128]{2,1,0:T(8,128)(2,1)}, f32[4,72,128]{2,1,0:T(8,128)}, s32[1,260]{1,0:T(1,128)}, s32[1,260]{1,0:T(1,128)}, /*index=5*/s32[1,1]{1,0:T(1,128)}) custom-call(bf16[8,80,128]{2,1,0:T(8,128)(2,1)} %copy-done, bf16[64,192,128]{2,1,0:T(8,128)(2,1)} %pad.4.passages, s32[1,64]{1,0:T(1,128)} %bitcast.16, ...), custom_call_target="tpu_custom_call" | custom-call | tf_op jit(solution)/shard_map/score/pallas_call | solution.py:366
  36.4 1.0 reshape.15
  37.4 15.6 %all_to_all.15 = f32[8,1,1536]{2,1,0:T(1,128)S(1)} all-to-all(f32[8,1,1536]{2,1,0:T(1,128)S(1)} %reshape.15), channel_id=1, replica_groups=mesh['grp'=8,'rep'=4] {'grp'}, dimensions={0} | all-to-all | bytes 98304 | tf_op jit(solution)/shard_map/all_to_all | solution.py:387
  53.1 0.5 broadcast.2
  53.6 0.8 reduce
  54.3 0.7 reshape.16.scores
  55.1 18.4 %query_grad.1 = (bf16[8,64,128]{2,1,0:T(8,128)(2,1)}, bf16[260,192,128]{2,1,0:T(8,128)(2,1)}, f32[8,128]{1,0:T(8,128)}) custom-call(bf16[8,80,128]{2,1,0:T(8,128)(2,1)} %copy-done, f32[8,24,64]{2,1,0:T(8,128)} %reshape.16.scores, bf16[64,192,128]{2,1,0:T(8,128)(2,1)} %pad.4.passages, ...), custom_call_target="tpu_custom_call", output_to_operand_aliasing={{1}: (4, {})} | custom-call | tf_op jit(solution)/shard_map/query_grad/pallas_call | solution.py:390
  73.5 6.4 %all-to-all-start.2 = ((bf16[8,64,128]{2,1,0:T(8,128)(2,1)}), bf16[8,64,128]{2,1,0:T(8,128)(2,1)S(1)}, u32[]{:S(2)}, u32[]{:S(2)}) async-start(bf16[8,64,128]{2,1,0:T(8,128)(2,1)} %get-tuple-element.19), calls=%async_computation.2 | async-start | bytes 262144 | tf_op jit(solution)/shard_map/all_to_all | solution.py:406
  79.9 1.4 %fusion = (f32[1,1]{1,0:T(1,128)}, f32[1,1]{1,0:T(1,128)}) fusion(f32[8,128]{1,0:T(8,128)} %get-tuple-element.18), kind=kLoop, calls=%fused_computation.3 | loop fusion | bytes 16 | tf_op jit(solution)/shard_map/slice | solution.py:421
  81.2 0.0 collective-permute-start.2
  81.2 13.1 %passage_grad.1 = bf16[64,180,128]{2,1,0:T(8,128)(2,1)} custom-call(bf16[8,80,128]{2,1,0:T(8,128)(2,1)} %copy-done, bf16[260,192,128]{2,1,0:T(8,128)(2,1)} %get-tuple-element.20.scaled, s32[1,260]{1,0:T(1,128)} %get-tuple-element.15.block_row, s32[1,260]{1,0:T(1,128)} %get-tuple-element.16.block_tile, s32[1,1]{1,0:T(1,128)} %get-tuple-element.17.block_count), custom_call_target="tpu_custom_call" | custom-call | tf_op jit(solution)/shard_map/passage_grad/pallas_call | solution.py:408
  94.3 4.2 %copy.12 = bf16[64,1,180,128]{3,0,2,1:T(8,128)(2,1)} copy(bf16[64,1,180,128]{3,2,0,1:T(8,128)(2,1)} %bitcast.10) | data formatting | bytes 5898240
  98.6 0.0 collective-permute-done.2
  99.9 6.1 %collective-permute-start.3 = (f32[1,1]{1,0:T(1,128)}, f32[1,1]{1,0:T(1,128)}, u32[]{:S(2)}, u32[]{:S(2)}) collective-permute-start(f32[1,1]{1,0:T(1,128)} %add.16), channel_id=1, source_target_pairs={{0,2},{1,3},{2,0},{3,1},{4,6},{5,7},{6,4},{7,5},{8,10},{9,11},{10,... | collective-permute-start | bytes 20 | tf_op jit(solution)/shard_map/ppermute | solution.py:425
  106.0 0.4 collective-permute-done.3
  107.6 0.0 all-to-all-done.2
  107.6 0.6 convert_reduce_fusion
  (1 shorter events, 0.0 us)
Async XLA Ops:
  2.2 17.3 %all-to-all-start = ((bf16[8,80,128]{2,1,0:T(8,128)(2,1)}), bf16[8,80,128]{2,1,0:T(8,128)(2,1)S(1)}, u32[]{:S(2)}, u32[]{:S(2)}) async-start(bf16[8,80,128]{2,1,0:T(8,128)(2,1)} %pack.1), calls=%async_computation | async-start | bytes 327680 | tf_op jit(solution)/shard_map/all_to_all | solution.py:354
  9.5 5.9 %collective-permute-start = (f32[1,2]{1,0:T(1,128)}, f32[1,2]{1,0:T(1,128)S(1)}, u32[]{:S(2)}, u32[]{:S(2)}) collective-permute-start(f32[1,2]{1,0:T(1,128)} %bitcast.15), channel_id=1, source_target_pairs={{0,1},{1,0},{2,3},{3,2},{4,5},{5,4},{6,7},{7,6},{8,9},{9,8},{10,11... | collective-permute-start | bytes 32 | tf_op jit(solution)/shard_map/ppermute | solution.py:360
  13.3 2.1 %copy-start.1 = (f32[2,1]{0,1:T(1,128)S(1)}, f32[2,1]{0,1:T(1,128)}, u32[]{:S(2)}) copy-start(f32[2,1]{0,1:T(1,128)} %param.13) | copy-start | bytes 28
  15.4 3.6 %collective-permute-start.1 = (f32[1,2]{1,0:T(1,128)S(1)}, f32[1,2]{1,0:T(1,128)S(1)}, u32[]{:S(2)}, u32[]{:S(2)}) collective-permute-start(f32[1,2]{1,0:T(1,128)S(1)} %bitcast_add_fusion), channel_id=1, source_target_pairs={{0,2},{1,3},{2,0},{3,1},{4,6},{5,7},{6,4},{7,5},{8,10},{9,11},{10,... | collective-permute-start | bytes 32 | tf_op jit(solution)/shard_map/ppermute | solution.py:360
  19.6 0.7 copy-start
  73.5 34.1 %all-to-all-start.2 = ((bf16[8,64,128]{2,1,0:T(8,128)(2,1)}), bf16[8,64,128]{2,1,0:T(8,128)(2,1)S(1)}, u32[]{:S(2)}, u32[]{:S(2)}) async-start(bf16[8,64,128]{2,1,0:T(8,128)(2,1)} %get-tuple-element.19), calls=%async_computation.2 | async-start | bytes 262144 | tf_op jit(solution)/shard_map/all_to_all | solution.py:406
  81.2 17.3 %collective-permute-start.2 = (f32[1,1]{1,0:T(1,128)}, f32[1,1]{1,0:T(1,128)}, u32[]{:S(2)}, u32[]{:S(2)}) collective-permute-start(f32[1,1]{1,0:T(1,128)} %get-tuple-element.25), channel_id=1, source_target_pairs={{0,1},{1,0},{2,3},{3,2},{4,5},{5,4},{6,7},{7,6},{8,9},{9,8},{10,11... | collective-permute-start | bytes 20 | tf_op jit(solution)/shard_map/ppermute | solution.py:425
  99.9 6.4 %collective-permute-start.3 = (f32[1,1]{1,0:T(1,128)}, f32[1,1]{1,0:T(1,128)}, u32[]{:S(2)}, u32[]{:S(2)}) collective-permute-start(f32[1,1]{1,0:T(1,128)} %add.16), channel_id=1, source_target_pairs={{0,2},{1,3},{2,0},{3,1},{4,6},{5,7},{6,4},{7,5},{8,10},{9,11},{10,... | collective-permute-start | bytes 20 | tf_op jit(solution)/shard_map/ppermute | solution.py:425

commit v2 on v1

v2 whole, which is shorter than its diff:
```python
import functools
import math

import jax
import jax.numpy as jnp
from jax import lax
from jax.experimental import pallas as pl
from jax.experimental.pallas import tpu as pltpu
from jax.sharding import PartitionSpec as P

TEMPER = 0.05
LOG2E = math.log2(math.e)
MASKED = -1e30
KINDS = 8
UNROLL = 4
SPREAD = 4
HIGHEST = lax.Precision.HIGHEST
VMEM = pltpu.VMEM
SMEM = pltpu.SMEM


def round_up(value, multiple):
    return -(-value // multiple) * multiple


def iota(shape, dim):
    return lax.broadcasted_iota(jnp.int32, shape, dim)


def three_parts(values):
    first = values.astype(jnp.bfloat16).astype(jnp.float32)
    rest = values - first
    second = rest.astype(jnp.bfloat16).astype(jnp.float32)
    third = (rest - second).astype(jnp.bfloat16).astype(jnp.float32)
    return first, second, third


def pack_kernel(passage_local, queries, cand_ids, owner_map, teacher, weights, out, aux):
    groups = out.shape[0]
    tokens = queries.shape[0]
    query_local, _, candidates = cand_ids.shape
    entries = owner_map.shape[1]
    table = owner_map[...].astype(jnp.float32)
    owner = jnp.floor((table + 0.5) * (1.0 / passage_local))
    local = table - owner * passage_local
    which = iota((8, entries), 0)
    tables = jnp.where(which == 0, owner, jnp.where(which == 1, local, 0.0)).astype(jnp.bfloat16)
    aux[...] = jnp.zeros_like(aux)
    for q in range(query_local):
        hot = (iota((entries, candidates), 0) == cand_ids[q]).astype(jnp.bfloat16)
        found = jnp.dot(tables, hot, preferred_element_type=jnp.float32)
        scores = teacher[q]
        shifted = scores - jnp.max(scores, axis=1, keepdims=True)
        log_teacher = shifted - jnp.log(jnp.sum(jnp.exp(shifted), axis=1, keepdims=True))
        weight = jnp.broadcast_to(weights[:, q : q + 1], (1, candidates))
        rows = (found[0:1], found[1:2], *three_parts(log_teacher), *three_parts(weight))
        for kind, row in enumerate(rows):
            at = kind * query_local + q
            aux[at : at + 1, 0:candidates] = row
    packed = aux[...].astype(jnp.bfloat16)
    for g in range(groups):
        out[g, 0:tokens, :] = queries[...]
        out[g, tokens:, :] = packed


def owned_rows(arrived, tokens, query_local, candidates, g, q, me):
    at = tokens + q
    owner = arrived[g, at : at + 1, 0:candidates].astype(jnp.float32)
    at = tokens + query_local + q
    local = arrived[g, at : at + 1, 0:candidates].astype(jnp.float32)
    return jnp.where(owner == me.astype(jnp.float32), local, -1.0).astype(jnp.int32)


def prepare_kernel(stored, rows_out, turned_out, gathered):
    token_len, chunk, feature = stored.shape
    padded = rows_out.shape[1]
    pitch = gathered.shape[0] // chunk
    for p in range(chunk):
        at = p * pitch + token_len
        gathered[at : (p + 1) * pitch, :] = jnp.zeros((pitch - token_len, feature), jnp.float32)

    def spread(j, carry):
        for u in range(SPREAD):
            at = j * SPREAD + u
            gathered[pl.ds(at, chunk, stride=pitch), :] = stored[at].astype(jnp.float32)
        return carry

    lax.fori_loop(0, token_len // SPREAD, spread, 0)
    for j in range(token_len - token_len % SPREAD, token_len):
        gathered[pl.ds(j, chunk, stride=pitch), :] = stored[j].astype(jnp.float32)

    for p in range(chunk):
        block = gathered[p * pitch : p * pitch + padded, :].astype(jnp.bfloat16)
        rows_out[p] = block
        turned_out[p, :, 0:padded] = block.T


def list_blocks(flags_scalar, block_row, block_tile, block_count, passage_count, tiles):
    def list_passage(p, count):
        for tile in range(tiles):
            block_row[0, count] = p
            block_tile[0, count] = tile
            count = count + flags_scalar[p, tile]
        return count

    count = lax.fori_loop(0, passage_count, list_passage, jnp.int32(0))
    for extra in range(3 * UNROLL):
        block_row[0, count + extra] = passage_count
        block_tile[0, count + extra] = 0
    steps = (count + 2 * UNROLL - 1) // (2 * UNROLL)
    block_count[0, 0] = steps
    return steps


def score_kernel(
    dims,
    axis,
    arrived,
    lengths,
    passages_hbm,
    scores_out,
    highest,
    summed,
    weight_sum,
    block_row,
    block_tile,
    block_count,
    powers_hbm,
    passages,
    turned,
    flags,
    flags_scalar,
    penalty,
    even,
    odd,
    powers,
    flags_done,
    rows_done,
    powers_done,
):
    tokens, query_local, candidates, per_tile = dims
    groups = arrived.shape[0]
    passage_count, padded, feature = passages.shape
    tiles, _, lanes = highest.shape
    me = lax.axis_index(axis)
    groups_per_tile = per_tile // query_local
    fetch_rows = pltpu.make_async_copy(passages_hbm, passages, rows_done)
    fetch_rows.start()

    column = iota(flags.shape, 1)
    passage_index = iota((passage_count, candidates), 0)
    marks = jnp.zeros(flags.shape, jnp.int32)
    for tile in range(tiles):
        hit = jnp.zeros((passage_count, candidates), jnp.int32)
        for g in range(tile * groups_per_tile, (tile + 1) * groups_per_tile):
            for q in range(query_local):
                mine = owned_rows(arrived, tokens, query_local, candidates, g, q, me)
                hit = jnp.where(passage_index == mine, 1, hit)
        any_hit = jnp.max(hit, axis=1, keepdims=True)
        marks = jnp.where(column == tile, any_hit, marks)
    flags[...] = marks
    to_scalar = pltpu.make_async_copy(flags, flags_scalar, flags_done)
    to_scalar.start()

    total = jnp.zeros((1, 1), jnp.float32)
    for g in range(groups):
        for q in range(query_local):
            for part in range(5, 8):
                at = tokens + part * query_local + q
                total = total + arrived[g, at : at + 1, 0:1].astype(jnp.float32)
    weight_sum[...] = jnp.broadcast_to(total, weight_sum.shape)
    for tile in range(tiles):
        parts = [
            arrived[g, 0:tokens, :]
            for g in range(tile * groups_per_tile, (tile + 1) * groups_per_tile)
        ]
        block = jnp.concatenate(parts, axis=0).astype(jnp.float32)
        turned[tile] = block.T.astype(jnp.bfloat16)
    highest[...] = jnp.zeros_like(highest)
    summed[...] = jnp.ones_like(summed)
    penalty[...] = jnp.where(iota(penalty.shape, 0) < padded, 0.0, MASKED)
    to_scalar.wait()
    steps = list_blocks(flags_scalar, block_row, block_tile, block_count, passage_count, tiles)
    fetch_rows.wait()

    factor = LOG2E / TEMPER

    def multiply(first, into):
        for u in range(UNROLL):
            p = jnp.minimum(block_row[0, first + u], passage_count - 1)
            tile = block_tile[0, first + u]
            into[u] = jnp.dot(passages[p], turned[tile], preferred_element_type=jnp.float32)

    def soften(first, held):
        for u in range(UNROLL):
            slot = block_row[0, first + u]
            tile = block_tile[0, first + u]
            length = lengths[0, jnp.minimum(slot, passage_count - 1)]
            products = held[u] + penalty[pl.ds(padded - length, padded), :]
            top = jnp.max(products, axis=0, keepdims=True)
            raised = jnp.exp2((products - top) * factor)
            powers[first + u] = raised.astype(jnp.bfloat16)
            highest[tile, pl.ds(slot, 1), :] = top
            summed[tile, pl.ds(slot, 1), :] = jnp.sum(raised, axis=0, keepdims=True)

    def chunk_copy(s):
        at = pl.ds(s * 2 * UNROLL, 2 * UNROLL)
        return pltpu.make_async_copy(powers.at[at], powers_hbm.at[at], powers_done.at[s])

    multiply(0, even)

    def step(s, carry):
        first = s * 2 * UNROLL
        multiply(first + UNROLL, odd)
        soften(first, even)
        multiply(first + 2 * UNROLL, even)
        soften(first + UNROLL, odd)
        chunk_copy(s).start()
        return carry

    lax.fori_loop(0, steps, step, 0)

    query_len = lanes // per_tile
    member = iota((lanes, 128), 0) // query_len == iota((lanes, 128), 1)
    member = member.astype(jnp.float32)
    scores_out[0] = jnp.zeros(scores_out.shape[1:], jnp.float32)
    for tile in range(tiles):
        matched = highest[tile, 0:passage_count, :] + TEMPER * jnp.log(
            summed[tile, 0:passage_count, :]
        )
        sums = jnp.dot(matched, member, precision=HIGHEST, preferred_element_type=jnp.float32)
        for inner in range(per_tile):
            g = tile * groups_per_tile + inner // query_local
            q = inner % query_local
            mine = owned_rows(arrived, tokens, query_local, candidates, g, q, me)
            picked = jnp.where(passage_index == mine, sums[:, inner : inner + 1], 0.0)
            at = tile * per_tile + inner
            scores_out[0, at : at + 1, 0:candidates] = jnp.sum(picked, axis=0, keepdims=True)
    for g in range(1, groups):
        scores_out[g] = scores_out[0]

    def finish(s, carry):
        chunk_copy(s).wait()
        return carry

    lax.fori_loop(0, steps, finish, 0)


def query_kernel(
    dims,
    axis,
    arrived,
    scores,
    summed,
    weight_sum,
    block_row,
    block_tile,
    block_count,
    turned_hbm,
    powers_hbm,
    grads_out,
    multiplier,
    numerator_out,
    turned,
    powers,
    sums,
    turned_done,
    powers_done,
):
    tokens, query_local, candidates, per_tile, query_total = dims
    groups = arrived.shape[0]
    tiles, slots, lanes = summed.shape
    passage_count, _, padded = turned.shape
    padded = powers.shape[1]
    groups_per_tile = per_tile // query_local
    queries_all = tiles * per_tile
    query_len = lanes // per_tile
    me = lax.axis_index(axis)
    steps = block_count[0, 0]

    fetch_turned = pltpu.make_async_copy(turned_hbm, turned, turned_done)
    fetch_turned.start()

    def chunk_copy(s):
        at = pl.ds(s * 2 * UNROLL, 2 * UNROLL)
        return pltpu.make_async_copy(powers_hbm.at[at], powers.at[at], powers_done.at[s])

    def fetch(s, carry):
        chunk_copy(s).start()
        return carry

    lax.fori_loop(0, steps, fetch, 0)

    got = scores[0]
    for g in range(1, groups):
        got = got + scores[g]
    student = got[0:queries_all, 0:candidates]

    def gather_parts(kind):
        rows = []
        for g in range(groups):
            parts = []
            for part in range(3):
                at = tokens + (kind + part) * query_local
                block = arrived[g, at : at + query_local, 0:candidates]
                parts.append(block.astype(jnp.float32))
            rows.append((parts[0] + parts[1]) + parts[2])
        return jnp.concatenate(rows, axis=0)

    log_teacher = gather_parts(2)
    weight = gather_parts(5)
    shifted = student - jnp.max(student, axis=1, keepdims=True)
    log_student = shifted - jnp.log(jnp.sum(jnp.exp(shifted), axis=1, keepdims=True))
    teacher_prob = jnp.exp(log_teacher)
    spread = jnp.sum(weight * teacher_prob * (log_teacher - log_student), axis=1, keepdims=True)
    numerator = jnp.sum(spread, axis=0, keepdims=True)
    numerator_out[...] = jnp.broadcast_to(numerator, numerator_out.shape)
    scale = query_total / weight_sum[0:1, 0:1]
    grad = (weight * scale) * (jnp.exp(log_student) - teacher_prob)

    passage_index = iota((passage_count, candidates), 0)
    lane_query = iota((passage_count, lanes), 1) // query_len
    for tile in range(tiles):
        spread_out = jnp.zeros((passage_count, lanes), jnp.float32)
        for inner in range(per_tile):
            g = tile * groups_per_tile + inner // query_local
            q = inner % query_local
            mine = owned_rows(arrived, tokens, query_local, candidates, g, q, me)
            at = tile * per_tile + inner
            picked = jnp.where(passage_index == mine, grad[at : at + 1], 0.0)
            total = jnp.sum(picked, axis=1, keepdims=True)
            spread_out = jnp.where(lane_query == inner, total, spread_out)
        multiplier[tile, 0:passage_count, :] = spread_out / summed[tile, 0:passage_count, :]
        multiplier[tile, passage_count:, :] = jnp.zeros((slots - passage_count, lanes), jnp.float32)

    sums[...] = jnp.zeros_like(sums)
    fetch_turned.wait()

    def step(s, carry):
        chunk_copy(s).wait()
        for u in range(2 * UNROLL):
            b = s * 2 * UNROLL + u
            slot = block_row[0, b]
            tile = block_tile[0, b]
            p = jnp.minimum(slot, passage_count - 1)
            part = powers[b].astype(jnp.float32) * multiplier[tile, pl.ds(slot, 1), :]
            part = part.astype(jnp.bfloat16)
            sums[tile] += jnp.dot(
                turned[p, :, 0:padded], part, preferred_element_type=jnp.float32
            )
        return carry

    lax.fori_loop(0, steps, step, 0)
    for tile in range(tiles):
        back = sums[tile].T.astype(jnp.bfloat16)
        for inner in range(groups_per_tile):
            g = tile * groups_per_tile + inner
            grads_out[g] = back[inner * tokens : (inner + 1) * tokens]


def passage_kernel(
    dims,
    arrived,
    multiplier,
    block_row,
    block_tile,
    block_count,
    powers_hbm,
    out,
    powers,
    sums,
    queries_all,
    powers_done,
):
    tokens, per_tile_groups = dims
    token_len, passage_count, feature = out.shape
    tiles = queries_all.shape[0]
    padded = powers.shape[1]
    pitch = sums.shape[0] // (passage_count + 1)
    steps = block_count[0, 0]

    def chunk_copy(s):
        at = pl.ds(s * 2 * UNROLL, 2 * UNROLL)
        return pltpu.make_async_copy(powers_hbm.at[at], powers.at[at], powers_done.at[s])

    def fetch(s, carry):
        chunk_copy(s).start()
        return carry

    lax.fori_loop(0, steps, fetch, 0)
    for tile in range(tiles):
        for inner in range(per_tile_groups):
            g = tile * per_tile_groups + inner
            queries_all[tile, inner * tokens : (inner + 1) * tokens, :] = arrived[g, 0:tokens, :]

    def clear(p, carry):
        sums[pl.ds(p * pitch, pitch), :] = jnp.zeros((pitch, feature), jnp.float32)
        return carry

    lax.fori_loop(0, passage_count, clear, 0)

    def step(s, carry):
        chunk_copy(s).wait()
        for u in range(2 * UNROLL):
            b = s * 2 * UNROLL + u
            slot = block_row[0, b]
            tile = block_tile[0, b]
            part = powers[b].astype(jnp.float32) * multiplier[tile, pl.ds(slot, 1), :]
            at = pl.ds(pl.multiple_of(slot * pitch, 8), padded)
            sums[at, :] += jnp.dot(
                part.astype(jnp.bfloat16), queries_all[tile], preferred_element_type=jnp.float32
            )
        return carry

    lax.fori_loop(0, steps, step, 0)

    def store(j, carry):
        for u in range(SPREAD):
            at = j * SPREAD + u
            out[at] = sums[pl.ds(at, passage_count, stride=pitch), :].astype(out.dtype)
        return carry

    lax.fori_loop(0, token_len // SPREAD, store, 0)
    for j in range(token_len - token_len % SPREAD, token_len):
        out[j] = sums[pl.ds(j, passage_count, stride=pitch), :].astype(out.dtype)


def vmem(count):
    return [pl.BlockSpec(memory_space=VMEM)] * count


def smem(count):
    return [pl.BlockSpec(memory_space=SMEM)] * count


def over_replicas(values, replicas):
    hop = 1
    while hop < replicas:
        ring = [(r, r ^ hop) for r in range(replicas)]
        values = values + lax.ppermute(values, "rep", ring)
        hop *= 2
    return values


def hbm(count):
    return [pl.BlockSpec(memory_space=pltpu.HBM)] * count


def on_device(queries, passages, lengths, cand_ids, owner_map, teacher, weights):
    groups = lax.axis_size("grp")
    replicas = lax.axis_size("rep")
    query_local, _, query_len, feature = queries.shape
    passage_local, _, token_len, _ = passages.shape
    candidates = cand_ids.shape[2]
    tokens = query_local * query_len
    lanes = 128
    per_tile = lanes // query_len
    tiles = groups * tokens // lanes
    padded = round_up(token_len, 16)
    pitch = round_up(padded, 16) + 8
    ref_count = query_local * candidates
    capacity = groups * (2 * ref_count // groups)
    limit = min(passage_local * tiles, capacity)
    blocks = limit + 3 * UNROLL
    chunks = -(-limit // (2 * UNROLL))
    aux_rows = round_up(KINDS * query_local, 16)
    slots = round_up(passage_local + 1, 8)
    score_rows = round_up(groups * query_local, 8)
    shape = jax.ShapeDtypeStruct
    params = pltpu.CompilerParams(vmem_limit_bytes=36 * 2**20)

    share = pl.pallas_call(
        functools.partial(pack_kernel, passage_local),
        out_shape=shape((groups, tokens + aux_rows, feature), jnp.bfloat16),
        in_specs=vmem(5),
        out_specs=pl.BlockSpec(memory_space=VMEM),
        scratch_shapes=[VMEM((aux_rows, feature), jnp.float32)],
        name="pack",
        compiler_params=params,
    )(queries.reshape(tokens, feature), cand_ids, owner_map, teacher, weights.T)
    arrived = lax.all_to_all(share, "grp", split_axis=0, concat_axis=0, tiled=True)

    chunk = math.gcd(passage_local, 16)
    rows, turned = pl.pallas_call(
        prepare_kernel,
        grid=(passage_local // chunk,),
        out_shape=(
            shape((passage_local, padded, feature), jnp.bfloat16),
            shape((passage_local, feature, round_up(padded, 128)), jnp.bfloat16),
        ),
        in_specs=[pl.BlockSpec((token_len, chunk, feature), lambda i: (0, i, 0))],
        out_specs=(
            pl.BlockSpec((chunk, padded, feature), lambda i: (i, 0, 0)),
            pl.BlockSpec((chunk, feature, round_up(padded, 128)), lambda i: (i, 0, 0)),
        ),
        scratch_shapes=[VMEM((chunk * pitch, feature), jnp.float32)],
        name="prepare",
        compiler_params=params,
    )(passages[:, 0].transpose(1, 0, 2))

    dims = (tokens, query_local, candidates, per_tile)
    scores, highest, summed, weight_sum, block_row, block_tile, block_count, powers = (
        pl.pallas_call(
            functools.partial(score_kernel, dims, "grp"),
            out_shape=(
                shape((groups, score_rows, 128), jnp.float32),
                shape((tiles, slots, lanes), jnp.float32),
                shape((tiles, slots, lanes), jnp.float32),
                shape((1, 128), jnp.float32),
                shape((1, blocks), jnp.int32),
                shape((1, blocks), jnp.int32),
                shape((1, 1), jnp.int32),
                shape((chunks * 2 * UNROLL, padded, lanes), jnp.bfloat16),
            ),
            in_specs=vmem(1) + smem(1) + hbm(1),
            out_specs=tuple(vmem(4) + smem(3) + hbm(1)),
            scratch_shapes=[
                VMEM((passage_local, padded, feature), jnp.bfloat16),
                VMEM((tiles, feature, lanes), jnp.bfloat16),
                VMEM((passage_local, 128), jnp.int32),
                SMEM((passage_local, 128), jnp.int32),
                VMEM((2 * padded, lanes), jnp.float32),
                VMEM((UNROLL, padded, lanes), jnp.float32),
                VMEM((UNROLL, padded, lanes), jnp.float32),
                VMEM((chunks * 2 * UNROLL, padded, lanes), jnp.bfloat16),
                pltpu.SemaphoreType.DMA,
                pltpu.SemaphoreType.DMA,
                pltpu.SemaphoreType.DMA((chunks,)),
            ],
            name="score",
            compiler_params=params,
        )(arrived, lengths.T, rows)
    )
    all_scores = lax.all_to_all(scores, "grp", split_axis=0, concat_axis=0, tiled=True)
    weight_sum = over_replicas(weight_sum, replicas)

    query_total = query_local * groups * replicas
    grads, multiplier, numerator = pl.pallas_call(
        functools.partial(query_kernel, dims + (query_total,), "grp"),
        out_shape=(
            shape((groups, tokens, feature), jnp.bfloat16),
            shape((tiles, slots, lanes), jnp.float32),
            shape((1, 128), jnp.float32),
        ),
        in_specs=vmem(4) + smem(3) + hbm(2),
        out_specs=tuple(vmem(3)),
        scratch_shapes=[
            VMEM(turned.shape, jnp.bfloat16),
            VMEM(powers.shape, jnp.bfloat16),
            VMEM((tiles, feature, lanes), jnp.float32),
            pltpu.SemaphoreType.DMA,
            pltpu.SemaphoreType.DMA((chunks,)),
        ],
        name="query_grad",
        compiler_params=params,
    )(arrived, all_scores, summed, weight_sum, block_row, block_tile, block_count, turned, powers)
    returned = lax.all_to_all(grads, "grp", split_axis=0, concat_axis=0, tiled=True)

    passage_grad = pl.pallas_call(
        functools.partial(passage_kernel, (tokens, per_tile // query_local)),
        out_shape=shape((token_len, passage_local, feature), jnp.bfloat16),
        in_specs=vmem(2) + smem(3) + hbm(1),
        out_specs=pl.BlockSpec(memory_space=VMEM),
        scratch_shapes=[
            VMEM(powers.shape, jnp.bfloat16),
            VMEM(((passage_local + 1) * pitch, feature), jnp.float32),
            VMEM((tiles, lanes, feature), jnp.bfloat16),
            pltpu.SemaphoreType.DMA((chunks,)),
        ],
        name="passage_grad",
        compiler_params=params,
    )(arrived, multiplier, block_row, block_tile, block_count, powers)
    numerator = over_replicas(numerator, replicas)

    loss = numerator[0, 0] / weight_sum[0, 0]
    query_grad = jnp.sum(returned.astype(jnp.float32), axis=0)
    query_grad = query_grad.reshape(query_local, 1, query_len, feature)
    return (loss, query_grad, passage_grad.transpose(1, 0, 2)[:, None])


def solution(mesh):
    return jax.shard_map(
        on_device,
        mesh=mesh,
        in_specs=(
            P("grp", "rep", None, None),
            P("grp", "rep", None, None),
            P("grp", "rep"),
            P("grp", "rep", None),
            P("rep", None),
            P("grp", "rep", None),
            P("grp", "rep"),
        ),
        out_specs=(P(), P("grp", "rep", None, None), P("grp", "rep", None, None)),
        check_vma=False,
    )
```

time: 110 us -> 98.1 us (0.89)
  the two profiles are of different devices: /device:TPU:0 before, /device:TPU:18 now
where the time goes in v2:
time: 98.1 us; the launch traced here: 98.5 us
  Pallas kernels  49.9 us (51%)
  local copies, waits for them, and re-layouts  23 us (23%)
  starting transfers between devices  18.5 us (19%)
  waiting for transfers between devices  4.39 us (4%)
  between operations  1.95 us (2%)
    unnamed x24, local copies, waits for them, and re-layouts  23 us
    pallas_call x1, Pallas kernels, on_device(): pl.pallas_call(functools.partial(score_kernel, dims, 'grp'), out_shape=(s...  17.1 us
    pallas_call x1, Pallas kernels, on_device(): pl.pallas_call(functools.partial(passage_kernel, (tokens, per_tile // que...  14.6 us
    pallas_call x1, Pallas kernels, on_device(): pl.pallas_call(functools.partial(query_kernel, dims + (query_total,), 'gr...  13.6 us
    all_to_all x1, starting transfers between devices, on_device(): lax.all_to_all(share, 'grp', split_axis=0, concat_axis=0, tiled=True)  6.17 us
    ppermute x4, waiting for transfers between devices, over_replicas(): values = values + lax.ppermute(values, 'rep', ring)  4.39 us
    all_to_all x1, starting transfers between devices, on_device(): lax.all_to_all(grads, 'grp', split_axis=0, concat_axis=0, tiled=True)  4.21 us
    all_to_all x1, starting transfers between devices, on_device(): lax.all_to_all(scores, 'grp', split_axis=0, concat_axis=0, tiled=True)  4.2 us
  transfers between devices with their start and end apart: 7, of which 3 were waited for; matrix products, arithmetic and copies ran while one was open for 0% of the time, Pallas kernels for 19%

profile of v2, /device:TPU:18, one launch (start us, length us, event | category | flops | bytes accessed | tf_op | source)
XLA Modules:
  0.0 98.5 jit_solution(16830001039550016034)
XLA Ops:
  0.6 0.0 copy-start.11
  0.6 0.0 copy-start.6
  0.7 0.7 copy-done.6
  1.4 0.0 copy-start.7
  1.4 0.7 copy-done.7
  2.0 0.0 copy-start.8
  2.1 0.7 copy-done.8
  2.7 0.0 copy-start.9
  2.7 0.7 copy-done.9
  3.4 0.0 copy-start.10
  3.4 0.7 copy-done.10
  4.1 0.9 pack.1
  4.9 6.2 %all-to-all-start = ((bf16[8,80,128]{2,1,0:T(8,128)(2,1)}), bf16[8,80,128]{2,1,0:T(8,128)(2,1)S(1)}, u32[]{:S(2)}, u32[]{:S(2)}) async-start(bf16[8,80,128]{2,1,0:T(8,128)(2,1)} %pack.1), calls=%async_computation | async-start | bytes 327680 | tf_op jit(solution)/shard_map/all_to_all | solution.py:481
  11.1 0.0 copy-start.5
  11.1 1.8 %copy-done.5 = bf16[64,1,180,128]{3,0,2,1:T(8,128)(2,1)S(1)} copy-done((bf16[64,1,180,128]{3,0,2,1:T(8,128)(2,1)S(1)}, bf16[64,1,180,128]{3,0,2,1:T(8,128)(2,1)}, u32[]{:S(2)}) %copy-start.5) | copy-done | bytes 2949144
  12.9 3.7 %prepare.1 = (bf16[64,192,128]{2,1,0:T(8,128)(2,1)S(1)}, bf16[64,128,256]{2,1,0:T(8,128)(2,1)S(1)}) custom-call(bf16[180,64,128]{2,1,0:T(8,128)(2,1)S(1)} %bitcast.13), custom_call_target="tpu_custom_call" | custom-call | tf_op jit(solution)/shard_map/prepare/pallas_call | solution.py:484
  16.7 0.0 copy-start.3
  16.7 1.9 %copy-done.3 = bf16[64,128,256]{2,1,0:T(8,128)(2,1)} copy-done((bf16[64,128,256]{2,1,0:T(8,128)(2,1)}, bf16[64,128,256]{2,1,0:T(8,128)(2,1)S(1)}, u32[]{:S(2)}) %copy-start.3) | copy-done | bytes 4194328
  18.6 0.0 all-to-all-done.arrived
  18.6 0.0 copy-done.11
  18.6 17.1 %score.1 = (f32[8,16,128]{2,1,0:T(8,128)}, f32[4,72,128]{2,1,0:T(8,128)}, f32[4,72,128]{2,1,0:T(8,128)S(1)}, f32[1,128]{1,0:T(1,128)S(1)}, s32[1,268]{1,0:T(1,12...) custom-call(bf16[8,80,128]{2,1,0:T(8,128)(2,1)S(1)} %all-to-all-done.arrived, ...), custom_call_target="tpu_custom_call" | custom-call | tf_op jit(solution)/shard_map/score/pallas_call | solution.py:503
  35.8 0.0 copy-start
  35.8 4.5 %copy-done = bf16[256,192,128]{2,1,0:T(8,128)(2,1)} copy-done((bf16[256,192,128]{2,1,0:T(8,128)(2,1)}, bf16[256,192,128]{2,1,0:T(8,128)(2,1)S(1)}, u32[]{:S(2)}) %copy-start) | copy-done | bytes 12582936
  40.3 4.2 %all-to-all-start.1 = ((f32[8,16,128]{2,1,0:T(8,128)}), f32[8,16,128]{2,1,0:T(8,128)S(1)}, u32[]{:S(2)}, u32[]{:S(2)}) async-start(f32[8,16,128]{2,1,0:T(8,128)} %get-tuple-element.16), calls=%async_computation.1 | async-start | bytes 131072 | tf_op jit(solution)/shard_map/all_to_all | solution.py:534
  44.5 0.0 collective-permute-start
  44.5 1.2 %collective-permute-done = f32[1,128]{1,0:T(1,128)S(1)} collective-permute-done((f32[1,128]{1,0:T(1,128)S(1)}, f32[1,128]{1,0:T(1,128)S(1)}, u32[]{:S(2)}, u32[]{:S(2)}) %collective-permute-start) | collective-permute-done | bytes 544 | tf_op jit(solution)/shard_map/ppermute | solution.py:440
  45.7 1.5 %collective-permute-start.1 = (f32[1,128]{1,0:T(1,128)S(1)}, f32[1,128]{1,0:T(1,128)S(1)}, u32[]{:S(2)}, u32[]{:S(2)}) collective-permute-start(f32[1,128]{1,0:T(1,128)S(1)} %add.12), channel_id=1, source_target_pairs={{0,2},{1,3},{2,0},{3,1},{4,6},{5,7},{6,4},{7,5},{8,10},{9,11},{10,... | collective-permute-start | bytes 1544 | tf_op jit(solution)/shard_map/ppermute | solution.py:440
  47.2 2.1 %collective-permute-done.1 = f32[1,128]{1,0:T(1,128)S(1)} collective-permute-done((f32[1,128]{1,0:T(1,128)S(1)}, f32[1,128]{1,0:T(1,128)S(1)}, u32[]{:S(2)}, u32[]{:S(2)}) %collective-permute-start.1) | collective-permute-done | bytes 544 | tf_op jit(solution)/shard_map/ppermute | solution.py:440
  49.2 0.0 all-to-all-done.1.scores
  49.2 0.0 copy-start.1
  49.2 4.6 %copy-done.1 = bf16[256,192,128]{2,1,0:T(8,128)(2,1)S(1)} copy-done((bf16[256,192,128]{2,1,0:T(8,128)(2,1)S(1)}, bf16[256,192,128]{2,1,0:T(8,128)(2,1)}, u32[]{:S(2)}) %copy-start.1) | copy-done | bytes 12582936
  53.8 0.0 copy-start.4
  53.8 2.2 %copy-done.4 = bf16[64,128,256]{2,1,0:T(8,128)(2,1)S(1)} copy-done((bf16[64,128,256]{2,1,0:T(8,128)(2,1)S(1)}, bf16[64,128,256]{2,1,0:T(8,128)(2,1)}, u32[]{:S(2)}) %copy-start.4) | copy-done | bytes 4194328
  56.0 13.6 %query_grad.1 = (bf16[8,64,128]{2,1,0:T(8,128)(2,1)}, f32[4,72,128]{2,1,0:T(8,128)S(1)}, f32[1,128]{1,0:T(1,128)S(1)}) custom-call(bf16[8,80,128]{2,1,0:T(8,128)(2,1)S(1)} %all-to-all-done.arrived, f32[8,16,128]{2,1,0:T(8,128)S(1)} %all-to-all-done.1.scores, f32[4,72,128]{2,1,0:T(8,128)S(1)} %get-tuple-element.17.summed, f32[1,128]{1,0:T(1,128)S(1)} %add.13.weight_sum, ...), custom_call_target="tpu_custom_call" | custom-call | tf_op jit(solution)/shard_map/query_grad/pallas_call | solution.py:538
  69.6 4.2 %all-to-all-start.2 = ((bf16[8,64,128]{2,1,0:T(8,128)(2,1)}), bf16[8,64,128]{2,1,0:T(8,128)(2,1)S(1)}, u32[]{:S(2)}, u32[]{:S(2)}) async-start(bf16[8,64,128]{2,1,0:T(8,128)(2,1)} %get-tuple-element.25), calls=%async_computation.2 | async-start | bytes 262144 | tf_op jit(solution)/shard_map/all_to_all | solution.py:557
  73.8 0.0 collective-permute-start.2
  73.8 1.2 %collective-permute-done.2 = f32[1,128]{1,0:T(1,128)S(1)} collective-permute-done((f32[1,128]{1,0:T(1,128)S(1)}, f32[1,128]{1,0:T(1,128)S(1)}, u32[]{:S(2)}, u32[]{:S(2)}) %collective-permute-start.2) | collective-permute-done | bytes 544 | tf_op jit(solution)/shard_map/ppermute | solution.py:440
  75.0 2.4 %collective-permute-start.3 = (f32[1,128]{1,0:T(1,128)S(1)}, f32[1,128]{1,0:T(1,128)S(1)}, u32[]{:S(2)}, u32[]{:S(2)}) collective-permute-start(f32[1,128]{1,0:T(1,128)S(1)} %add.14), channel_id=1, source_target_pairs={{0,2},{1,3},{2,0},{3,1},{4,6},{5,7},{6,4},{7,5},{8,10},{9,11},{10,... | collective-permute-start | bytes 1544 | tf_op jit(solution)/shard_map/ppermute | solution.py:440
  77.4 0.0 copy-start.2
  77.4 4.6 %copy-done.2 = bf16[256,192,128]{2,1,0:T(8,128)(2,1)S(1)} copy-done((bf16[256,192,128]{2,1,0:T(8,128)(2,1)S(1)}, bf16[256,192,128]{2,1,0:T(8,128)(2,1)}, u32[]{:S(2)}) %copy-start.2) | copy-done | bytes 12582936
  82.0 14.6 %passage_grad.1 = bf16[180,64,128]{2,1,0:T(8,128)(2,1)} custom-call(bf16[8,80,128]{2,1,0:T(8,128)(2,1)S(1)} %all-to-all-done.arrived, f32[4,72,128]{2,1,0:T(8,128)S(1)} %get-tuple-element.26.multiplier, s32[1,268]{1,0:T(1,128)S(1)} %get-tuple-element.19.block_row, s32[1,268]{1,0:T(1,128)S(1)} %get-tuple-element.20.block_tile, ...), custom_call_target="tpu_custom_call" | custom-call | tf_op jit(solution)/shard_map/passage_grad/pallas_call | solution.py:559
  96.6 0.0 collective-permute-done.3
  96.7 0.0 all-to-all-done.2
  96.7 0.6 convert_reduce_fusion
  (4 shorter events, 0.0 us)
Async XLA Ops:
  0.6 18.0 %copy-start.11 = (s32[64,1]{0,1:T(1,128)S(1)}, s32[64,1]{0,1:T(1,128)}, u32[]{:S(2)}) copy-start(s32[64,1]{0,1:T(1,128)} %param.9) | copy-start | bytes 772
  0.6 0.7 copy-start.6
  1.4 0.7 copy-start.7
  2.0 0.7 copy-start.8
  2.7 0.7 copy-start.9
  3.4 0.7 copy-start.10
  4.9 13.7 %all-to-all-start = ((bf16[8,80,128]{2,1,0:T(8,128)(2,1)}), bf16[8,80,128]{2,1,0:T(8,128)(2,1)S(1)}, u32[]{:S(2)}, u32[]{:S(2)}) async-start(bf16[8,80,128]{2,1,0:T(8,128)(2,1)} %pack.1), calls=%async_computation | async-start | bytes 327680 | tf_op jit(solution)/shard_map/all_to_all | solution.py:481
  11.1 1.8 %copy-start.5 = (bf16[64,1,180,128]{3,0,2,1:T(8,128)(2,1)S(1)}, bf16[64,1,180,128]{3,0,2,1:T(8,128)(2,1)}, u32[]{:S(2)}) copy-start(bf16[64,1,180,128]{3,0,2,1:T(8,128)(2,1)} %param.8) | copy-start | bytes 8847364
  16.7 1.9 %copy-start.3 = (bf16[64,128,256]{2,1,0:T(8,128)(2,1)}, bf16[64,128,256]{2,1,0:T(8,128)(2,1)S(1)}, u32[]{:S(2)}) copy-start(bf16[64,128,256]{2,1,0:T(8,128)(2,1)S(1)} %get-tuple-element.22.turned_hbm) | copy-start | bytes 12582916
  35.8 4.5 %copy-start = (bf16[256,192,128]{2,1,0:T(8,128)(2,1)}, bf16[256,192,128]{2,1,0:T(8,128)(2,1)S(1)}, u32[]{:S(2)}) copy-start(bf16[256,192,128]{2,1,0:T(8,128)(2,1)S(1)} %get-tuple-element.23.powers_hbm) | copy-start | bytes 37748740
  40.3 8.9 %all-to-all-start.1 = ((f32[8,16,128]{2,1,0:T(8,128)}), f32[8,16,128]{2,1,0:T(8,128)S(1)}, u32[]{:S(2)}, u32[]{:S(2)}) async-start(f32[8,16,128]{2,1,0:T(8,128)} %get-tuple-element.16), calls=%async_computation.1 | async-start | bytes 131072 | tf_op jit(solution)/shard_map/all_to_all | solution.py:534
  44.5 1.2 %collective-permute-start = (f32[1,128]{1,0:T(1,128)S(1)}, f32[1,128]{1,0:T(1,128)S(1)}, u32[]{:S(2)}, u32[]{:S(2)}) collective-permute-start(f32[1,128]{1,0:T(1,128)S(1)} %get-tuple-element.18), channel_id=1, source_target_pairs={{0,1},{1,0},{2,3},{3,2},{4,5},{5,4},{6,7},{7,6},{8,9},{9,8},{10,11... | collective-permute-start | bytes 1544 | tf_op jit(solution)/shard_map/ppermute | solution.py:440
  45.7 3.6 %collective-permute-start.1 = (f32[1,128]{1,0:T(1,128)S(1)}, f32[1,128]{1,0:T(1,128)S(1)}, u32[]{:S(2)}, u32[]{:S(2)}) collective-permute-start(f32[1,128]{1,0:T(1,128)S(1)} %add.12), channel_id=1, source_target_pairs={{0,2},{1,3},{2,0},{3,1},{4,6},{5,7},{6,4},{7,5},{8,10},{9,11},{10,... | collective-permute-start | bytes 1544 | tf_op jit(solution)/shard_map/ppermute | solution.py:440
  49.2 4.6 %copy-start.1 = (bf16[256,192,128]{2,1,0:T(8,128)(2,1)S(1)}, bf16[256,192,128]{2,1,0:T(8,128)(2,1)}, u32[]{:S(2)}) copy-start(bf16[256,192,128]{2,1,0:T(8,128)(2,1)} %copy-done) | copy-start | bytes 37748740
  53.8 2.2 %copy-start.4 = (bf16[64,128,256]{2,1,0:T(8,128)(2,1)S(1)}, bf16[64,128,256]{2,1,0:T(8,128)(2,1)}, u32[]{:S(2)}) copy-start(bf16[64,128,256]{2,1,0:T(8,128)(2,1)} %copy-done.3) | copy-start | bytes 12582916
  69.6 27.1 %all-to-all-start.2 = ((bf16[8,64,128]{2,1,0:T(8,128)(2,1)}), bf16[8,64,128]{2,1,0:T(8,128)(2,1)S(1)}, u32[]{:S(2)}, u32[]{:S(2)}) async-start(bf16[8,64,128]{2,1,0:T(8,128)(2,1)} %get-tuple-element.25), calls=%async_computation.2 | async-start | bytes 262144 | tf_op jit(solution)/shard_map/all_to_all | solution.py:557
  73.8 1.2 %collective-permute-start.2 = (f32[1,128]{1,0:T(1,128)S(1)}, f32[1,128]{1,0:T(1,128)S(1)}, u32[]{:S(2)}, u32[]{:S(2)}) collective-permute-start(f32[1,128]{1,0:T(1,128)S(1)} %get-tuple-element.24), channel_id=1, source_target_pairs={{0,1},{1,0},{2,3},{3,2},{4,5},{5,4},{6,7},{7,6},{8,9},{9,8},{10,11... | collective-permute-start | bytes 1544 | tf_op jit(solution)/shard_map/ppermute | solution.py:440
  75.0 21.6 %collective-permute-start.3 = (f32[1,128]{1,0:T(1,128)S(1)}, f32[1,128]{1,0:T(1,128)S(1)}, u32[]{:S(2)}, u32[]{:S(2)}) collective-permute-start(f32[1,128]{1,0:T(1,128)S(1)} %add.14), channel_id=1, source_target_pairs={{0,2},{1,3},{2,0},{3,1},{4,6},{5,7},{6,4},{7,5},{8,10},{9,11},{10,... | collective-permute-start | bytes 1544 | tf_op jit(solution)/shard_map/ppermute | solution.py:440
  77.4 4.6 %copy-start.2 = (bf16[256,192,128]{2,1,0:T(8,128)(2,1)S(1)}, bf16[256,192,128]{2,1,0:T(8,128)(2,1)}, u32[]{:S(2)}) copy-start(bf16[256,192,128]{2,1,0:T(8,128)(2,1)} %copy-done) | copy-start | bytes 37748740
